TPU v7x, 32 devices: a whole 2x2x4 slice. The times are simulated.
32 devices in a mesh: panels: 32 (over z, y, x, core).
Axes of the slice: x: 2, y: 2, z: 4, core: 2. Of those that a mesh axis runs over, the one named last changes fastest.
Arguments:
- excitation: bfloat16 [64, 131072], P(None, 'panels'), may hold values from -6 to 6
- near_tiles: bfloat16 [512, 5, 256, 256], P('panels'), may hold values from -0.15625 to 0.15625
- near_offset: int32 [512, 5], P('panels'), may hold values from -16 to 16, as said below
- near_count: int32 [512], P('panels'), may hold values from 1 to 5, as said below
- far_src: int32 [32, 16], replicated, may hold values from 0 to 31, as said below
- far_count: int32 [32], replicated, may hold values from 1 to 16
- source_factor: bfloat16 [16, 32, 131072], P(None, None, 'panels'), may hold values from -0.09375 to 0.09375
- target_factor: bfloat16 [16, 32, 131072], P(None, None, 'panels'), may hold values from -0.25 to 0.25
Outputs:
- krylov: float32 [5, 64, 131072], P(None, None, 'panels')
Inputs may be any that keep to these rules, and one draw needn't show every extreme that they name: `near_offset`: offsets within one leaf are distinct. `near_count`: some leaf has 5 live slots. `far_src`: within a row the entries are distinct and never the row itself. Counting live slots only, every block row is the source of at most 16 far blocks, and some block row of exactly 16.
All inputs are finite; a program needn't handle non-finite values.
Results may differ from a plain program's by a relative error of at most 0.0095.
Values may be sent and summed in bfloat16 or wider, within the bound.
A program may use at most 128 MiB of HBM per device.

v0:
```python
import jax
import jax.numpy as jnp
from jax import lax
from jax.sharding import PartitionSpec as P

ITERS = 5


def extended_2(cells, sides, width):
    for axis, dim in sides:
        count = lax.axis_size(axis)
        head = lax.slice_in_dim(cells, 0, width, axis=dim)
        tail = lax.slice_in_dim(cells, cells.shape[dim] - width, cells.shape[dim], axis=dim)
        cells = jnp.concatenate(
            [
                lax.ppermute(tail, axis, [(i, (i + 1) % count) for i in range(count)]),
                cells,
                lax.ppermute(head, axis, [((i + 1) % count, i) for i in range(count)]),
            ],
            axis=dim,
        )
    return cells


def out_ranks(far_src, far_count):
    row_total, slot_count = far_src.shape
    live_far = jnp.arange(slot_count, dtype=jnp.int32)[None, :] < far_count[:, None]
    owners = jnp.arange(row_total, dtype=jnp.int32)
    hits = (
        (far_src.reshape(-1)[:, None] == owners[None, :]) & live_far.reshape(-1)[:, None]
    ).astype(jnp.int32)
    earlier = jnp.cumsum(hits, axis=0) - hits
    out_rank = jnp.sum(earlier * hits, axis=1)
    return (out_rank.reshape(row_total, slot_count), live_far)


def apply_operator(
    field,
    near_tiles,
    near_offset,
    near_count,
    far_src,
    out_rank,
    live_far,
    source_factor,
    target_factor,
):
    excite, panels_local = field.shape
    leaves_local, near_slots, leaf_size = (
        near_tiles.shape[0],
        near_tiles.shape[1],
        near_tiles.shape[2],
    )
    row_total, slot_count = far_src.shape
    padded = extended_2(field, (("panels", 1),), panels_local)
    extended = padded.reshape(excite, 3 * leaves_local, leaf_size)
    local_leaf = jnp.arange(leaves_local, dtype=jnp.int32)[:, None] + leaves_local + near_offset
    picked = jnp.take(extended, local_leaf.reshape(-1), axis=1)
    picked = picked.reshape(excite, leaves_local, near_slots, leaf_size)
    live_near = jnp.arange(near_slots, dtype=jnp.int32)[None, :] < near_count[:, None]
    picked = jnp.where(live_near[None, :, :, None], picked, jnp.zeros_like(picked))
    near_part = jnp.einsum("ijab,mijb->mia", near_tiles, picked, preferred_element_type=jnp.float32)
    near_part = near_part.reshape(excite, panels_local)
    own_index = lax.axis_index("panels")
    coeffs = jnp.einsum("jrp,mp->jrm", source_factor, field, preferred_element_type=jnp.float32)
    coeffs = coeffs.astype(jnp.bfloat16).reshape(slot_count, -1)
    own_src = lax.dynamic_index_in_dim(far_src, own_index, 0, keepdims=False)
    own_live = lax.dynamic_index_in_dim(live_far, own_index, 0, keepdims=False)
    mine = (far_src == own_index) & live_far
    placed = (
        out_rank[:, :, None] == jnp.arange(slot_count, dtype=jnp.int32)[None, None, :]
    ) & mine[:, :, None]
    selector = jnp.any(placed, axis=1).astype(jnp.bfloat16)
    outgoing = jnp.dot(selector, coeffs, preferred_element_type=jnp.float32).astype(jnp.bfloat16)
    received = lax.all_to_all(outgoing, "panels", split_axis=0, concat_axis=0, tiled=True)
    chooser = (own_src[:, None] == jnp.arange(row_total, dtype=jnp.int32)[None, :]) & own_live[
        :, None
    ]
    incoming = jnp.dot(chooser.astype(jnp.bfloat16), received, preferred_element_type=jnp.float32)
    rank_size = source_factor.shape[1]
    coef = incoming.astype(jnp.bfloat16).reshape(slot_count, rank_size, excite)
    far_part = jnp.einsum("jrm,jrp->mp", coef, target_factor, preferred_element_type=jnp.float32)
    return near_part + far_part


def shards(
    excitation,
    near_tiles,
    near_offset,
    near_count,
    far_src,
    far_count,
    source_factor,
    target_factor,
):
    out_rank, live_far = out_ranks(far_src, far_count)
    current = excitation
    results = []
    for step in range(ITERS):
        result = apply_operator(
            current,
            near_tiles,
            near_offset,
            near_count,
            far_src,
            out_rank,
            live_far,
            source_factor,
            target_factor,
        )
        results.append(result)
        current = result.astype(jnp.bfloat16)
    return jnp.stack(results, axis=0)


def solution(mesh):
    in_specs = (
        P(None, "panels"),
        P("panels", None, None, None),
        P("panels", None),
        P("panels"),
        P(),
        P(),
        P(None, None, "panels"),
        P(None, None, "panels"),
    )
    out_specs = P(None, None, "panels")
    return jax.shard_map(shards, mesh=mesh, in_specs=in_specs, out_specs=out_specs, check_vma=False)
```

profile of v0, /device:TPU:0, one launch (start us, length us, event | category | flops | bytes accessed | tf_op | source)
XLA Modules:
  0.0 177.6 jit_solution(6697552317192413001)
XLA Ops:
  0.0 6.4 %collective-permute-start.1 = (bf16[64,4096]{1,0:T(8,128)(2,1)}, bf16[64,4096]{1,0:T(8,128)(2,1)S(1)}, u32[]{:S(2)}, u32[]{:S(2)}) collective-permute-start(bf16[64,4096]{1,0:T(8,128)(2,1)} %param.10), channel_id=1, source_target_pairs={{1,0},{2,1},{3,2},{4,3},{5,4},{6,5},{7,6},{8,7},{9,8},{10,9},{11,1... | collective-permute-start | bytes 1572872 | tf_op jit(solution)/shard_map/ppermute | solution.py:18
  6.4 0.8 copy.96
  7.3 0.7 lt.108
  8.1 0.7 compare_and_fusion
  9.2 1.2 reduce-window.6
  11.0 3.6 %convolution_convert_fusion.14 = bf16[16,32,64]{2,1,0:T(8,128)(2,1)S(1)} fusion(bf16[16,32,4096]{2,1,0:T(8,128)(2,1)} %param.16, bf16[64,4096]{1,0:T(8,128)(2,1)} %param.10), kind=kOutput, calls=%fused_computation.76 | convolution fusion | flops 268468224 | bytes 4784128 | tf_op jit(solution)/shard_map/jrp,mp->jrm/dot_general | solution.py:65
  16.2 0.7 reshape.270
  16.9 5.7 %all-to-all-start = ((bf16[32,2,1024]{2,1,0:T(2,128)(2,1)}), bf16[32,2,1024]{2,1,0:T(2,128)(2,1)S(1)}, u32[]{:S(2)}, u32[]{:S(2)}) async-start(bf16[32,2,1024]{2,1,0:T(2,128)(2,1)} %reshape.270), calls=%async_computation | async-start | bytes 262144 | tf_op jit(solution)/shard_map/all_to_all | solution.py:75
  23.3 7.5 %all-to-all-done = bf16[32,2,1024]{2,1,0:T(2,128)(2,1)S(1)} async-done(((bf16[32,2,1024]{2,1,0:T(2,128)(2,1)}), bf16[32,2,1024]{2,1,0:T(2,128)(2,1)S(1)}, u32[]{:S(2)}, u32[]{:S(2)}) %all-to-all-start) | async-done | bytes 131104 | tf_op jit(solution)/shard_map/all_to_all | solution.py:75
  31.7 2.4 %gather_fusion = bf16[80,64,256]{2,1,0:T(8,128)(2,1)} fusion(bf16[64,48,256]{2,0,1:T(8,128)(2,1)S(1)} %bitcast.204, s32[1024]{0:T(1024)S(1)} %pad_clamp_fusion), kind=kCustom, calls=%fused_computation.clone | custom fusion | bytes 5243200 | tf_op jit(solution)/shard_map/jit(_take)/gather | solution.py:58
  34.1 2.0 %broadcast_select_fusion.4 = bf16[80,64,256]{2,1,0:T(8,128)(2,1)S(1)} fusion(bf16[80,64,256]{2,1,0:T(8,128)(2,1)} %gather_fusion, pred[80]{0:T(512)(128)(4,1)S(1)} %compare_and_fusion.1), kind=kLoop, calls=%fused_computation.31 | loop fusion | flops 1310720 | bytes 5242960 | tf_op jit(solution)/shard_map/jit(_take)/select_n | solution.py:58
  36.1 7.4 %fusion.27 = f32[16,8,8,256]{3,2,1,0:T(8,128)S(1)} fusion(bf16[16,5,256,256]{3,2,1,0:T(8,128)(2,1)} %param.11, bf16[64,16,5,256]{3,0,2,1:T(8,128)(2,1)S(1)} %bitcast.209, pred[16,5]{1,0:T(8,128)(4,1)S(1)} %iota_compare_fusion.5), kind=kOutput, calls=%fused_computation.62 | convolution fusion | flops 672399360 | bytes 14155856 | tf_op jit(solution)/shard_map/ijab,mijb->mia/dot_general | solution.py:62
  43.7 1.9 %bitcast_dynamic-update-slice_fusion.3 = (f32[5,64,4096]{2,1,0:T(8,128)}, bf16[64,4096]{1,0:T(8,128)(2,1)S(1)}) fusion(f32[64,4096]{1,0:T(8,128)S(1)} %bitcast.222, bf16[16,32,64]{2,1,0:T(8,128)(2,1)S(1)} %reshape.176, bf16[16,32,4096]{2,1,0:T(8,128)(2,1)S(1)} %copy-done.4), kind=kOutput, calls=%fused_computation.84 | convolution fusion | flops 268959744 | bytes 6881280 | tf_op jit(solution)/shard_map/jrm,jrp->mp/dot_general | solution.py:82
  45.5 0.7 copy-done
  46.2 1.2 fusion.47
  47.5 1.2 collective-permute-start.3
  49.1 0.6 reduce.7
  49.9 13.7 %all_to_all.60 = bf16[32,2,1024]{2,1,0:T(2,128)(2,1)S(1)} all-to-all(bf16[32,2,1024]{2,1,0:T(2,128)(2,1)S(1)} %reshape.272), channel_id=1, replica_groups=mesh['panels'=32] {'panels'}, dimensions={0} | all-to-all | bytes 262144 | tf_op jit(solution)/shard_map/all_to_all | solution.py:75
  64.4 2.4 %gather_fusion.1 = bf16[80,64,256]{2,1,0:T(8,128)(2,1)} fusion(bf16[64,48,256]{2,0,1:T(8,128)(2,1)S(1)} %bitcast.205, s32[1024]{0:T(1024)S(1)} %pad_clamp_fusion), kind=kCustom, calls=%fused_computation.1.clone | custom fusion | bytes 5243200 | tf_op jit(solution)/shard_map/jit(_take)/gather | solution.py:58
  66.8 2.0 %broadcast_select_fusion.3 = bf16[80,64,256]{2,1,0:T(8,128)(2,1)S(1)} fusion(bf16[80,64,256]{2,1,0:T(8,128)(2,1)} %gather_fusion.1, pred[80]{0:T(512)(128)(4,1)S(1)} %compare_and_fusion.1), kind=kLoop, calls=%fused_computation.30 | loop fusion | flops 1310720 | bytes 5242960 | tf_op jit(solution)/shard_map/jit(_take)/select_n | solution.py:58
  68.9 7.4 %fusion.30 = f32[16,8,8,256]{3,2,1,0:T(8,128)S(1)} fusion(bf16[16,5,256,256]{3,2,1,0:T(8,128)(2,1)} %param.11, bf16[64,16,5,256]{3,0,2,1:T(8,128)(2,1)S(1)} %bitcast.210, pred[16,5]{1,0:T(8,128)(4,1)S(1)} %iota_compare_fusion.5), kind=kOutput, calls=%fused_computation.63 | convolution fusion | flops 672399360 | bytes 14155856 | tf_op jit(solution)/shard_map/ijab,mijb->mia/dot_general | solution.py:62
  76.4 1.9 %bitcast_dynamic-update-slice_fusion.2 = (f32[5,64,4096]{2,1,0:T(8,128)}, bf16[64,4096]{1,0:T(8,128)(2,1)S(1)}) fusion(f32[5,64,4096]{2,1,0:T(8,128)} %get-tuple-element.8, f32[64,4096]{1,0:T(8,128)S(1)} %bitcast.219, bf16[16,32,64]{2,1,0:T(8,128)(2,1)S(1)} %reshape.181, bf16[16,32,4096]{2,1,0:T(8,128)(2,1)S(1)} %copy-done.5), kind=kOutput, calls=%fused_computation.83 | convolution fusion | flops 268959744 | bytes 6881280 | tf_op jit(solution)/shard_map/jrm,jrp->mp/dot_general | solution.py:82
  78.3 0.7 copy-done.1
  79.0 1.2 fusion.48
  80.2 1.7 collective-permute-start.5
  82.3 0.6 reduce.8
  83.1 13.9 %all_to_all.61 = bf16[32,2,1024]{2,1,0:T(2,128)(2,1)S(1)} all-to-all(bf16[32,2,1024]{2,1,0:T(2,128)(2,1)S(1)} %reshape.274), channel_id=1, replica_groups=mesh['panels'=32] {'panels'}, dimensions={0} | all-to-all | bytes 262144 | tf_op jit(solution)/shard_map/all_to_all | solution.py:75
  97.8 2.4 %gather_fusion.2 = bf16[80,64,256]{2,1,0:T(8,128)(2,1)} fusion(bf16[64,48,256]{2,0,1:T(8,128)(2,1)S(1)} %bitcast.206, s32[1024]{0:T(1024)S(1)} %pad_clamp_fusion), kind=kCustom, calls=%fused_computation.2.clone | custom fusion | bytes 5243200 | tf_op jit(solution)/shard_map/jit(_take)/gather | solution.py:58
  100.2 2.0 %broadcast_select_fusion.2 = bf16[80,64,256]{2,1,0:T(8,128)(2,1)S(1)} fusion(bf16[80,64,256]{2,1,0:T(8,128)(2,1)} %gather_fusion.2, pred[80]{0:T(512)(128)(4,1)S(1)} %compare_and_fusion.1), kind=kLoop, calls=%fused_computation.29 | loop fusion | flops 1310720 | bytes 5242960 | tf_op jit(solution)/shard_map/jit(_take)/select_n | solution.py:58
  102.3 7.4 %fusion.33 = f32[16,8,8,256]{3,2,1,0:T(8,128)S(1)} fusion(bf16[16,5,256,256]{3,2,1,0:T(8,128)(2,1)} %param.11, bf16[64,16,5,256]{3,0,2,1:T(8,128)(2,1)S(1)} %bitcast.211, pred[16,5]{1,0:T(8,128)(4,1)S(1)} %iota_compare_fusion.5), kind=kOutput, calls=%fused_computation.64 | convolution fusion | flops 672399360 | bytes 14155856 | tf_op jit(solution)/shard_map/ijab,mijb->mia/dot_general | solution.py:62
  109.8 1.9 %bitcast_dynamic-update-slice_fusion.1 = (f32[5,64,4096]{2,1,0:T(8,128)}, bf16[64,4096]{1,0:T(8,128)(2,1)S(1)}) fusion(f32[5,64,4096]{2,1,0:T(8,128)} %get-tuple-element.10, f32[64,4096]{1,0:T(8,128)S(1)} %bitcast.220, bf16[16,32,64]{2,1,0:T(8,128)(2,1)S(1)} %reshape.186, bf16[16,32,4096]{2,1,0:T(8,128)(2,1)S(1)} %copy-done.6), kind=kOutput, calls=%fused_computation.82 | convolution fusion | flops 268959744 | bytes 6881280 | tf_op jit(solution)/shard_map/jrm,jrp->mp/dot_general | solution.py:82
  111.7 0.7 copy-done.2
  112.4 1.2 fusion.49
  113.6 1.3 collective-permute-start.7
  115.3 0.6 reduce.9
  116.0 13.7 %all_to_all.62 = bf16[32,2,1024]{2,1,0:T(2,128)(2,1)S(1)} all-to-all(bf16[32,2,1024]{2,1,0:T(2,128)(2,1)S(1)} %reshape.276), channel_id=1, replica_groups=mesh['panels'=32] {'panels'}, dimensions={0} | all-to-all | bytes 262144 | tf_op jit(solution)/shard_map/all_to_all | solution.py:75
  130.6 2.4 %gather_fusion.3 = bf16[80,64,256]{2,1,0:T(8,128)(2,1)} fusion(bf16[64,48,256]{2,0,1:T(8,128)(2,1)S(1)} %bitcast.207, s32[1024]{0:T(1024)S(1)} %pad_clamp_fusion), kind=kCustom, calls=%fused_computation.3.clone | custom fusion | bytes 5243200 | tf_op jit(solution)/shard_map/jit(_take)/gather | solution.py:58
  133.0 2.0 %broadcast_select_fusion.1 = bf16[80,64,256]{2,1,0:T(8,128)(2,1)S(1)} fusion(bf16[80,64,256]{2,1,0:T(8,128)(2,1)} %gather_fusion.3, pred[80]{0:T(512)(128)(4,1)S(1)} %compare_and_fusion.1), kind=kLoop, calls=%fused_computation.28 | loop fusion | flops 1310720 | bytes 5242960 | tf_op jit(solution)/shard_map/jit(_take)/select_n | solution.py:58
  135.1 7.4 %fusion.36 = f32[16,8,8,256]{3,2,1,0:T(8,128)S(1)} fusion(bf16[16,5,256,256]{3,2,1,0:T(8,128)(2,1)} %param.11, bf16[64,16,5,256]{3,0,2,1:T(8,128)(2,1)S(1)} %bitcast.212, pred[16,5]{1,0:T(8,128)(4,1)S(1)} %iota_compare_fusion.5), kind=kOutput, calls=%fused_computation.65 | convolution fusion | flops 672399360 | bytes 14155856 | tf_op jit(solution)/shard_map/ijab,mijb->mia/dot_general | solution.py:62
  142.6 1.9 %bitcast_dynamic-update-slice_fusion = (f32[5,64,4096]{2,1,0:T(8,128)}, bf16[64,4096]{1,0:T(8,128)(2,1)S(1)}) fusion(f32[5,64,4096]{2,1,0:T(8,128)} %get-tuple-element.12, f32[64,4096]{1,0:T(8,128)S(1)} %bitcast.221, bf16[16,32,64]{2,1,0:T(8,128)(2,1)S(1)} %reshape.191, bf16[16,32,4096]{2,1,0:T(8,128)(2,1)S(1)} %copy-done.7), kind=kOutput, calls=%fused_computation.81 | convolution fusion | flops 268959744 | bytes 6881280 | tf_op jit(solution)/shard_map/jrm,jrp->mp/dot_general | solution.py:82
  144.5 0.7 copy-done.3
  145.2 1.2 fusion.50
  146.4 1.5 collective-permute-start.9
  149.1 13.8 %all_to_all.63 = bf16[32,2,1024]{2,1,0:T(2,128)(2,1)S(1)} all-to-all(bf16[32,2,1024]{2,1,0:T(2,128)(2,1)S(1)} %reshape.278), channel_id=1, replica_groups=mesh['panels'=32] {'panels'}, dimensions={0} | all-to-all | bytes 262144 | tf_op jit(solution)/shard_map/all_to_all | solution.py:75
  163.8 2.4 %gather_fusion.4 = bf16[80,64,256]{2,1,0:T(8,128)(2,1)} fusion(bf16[64,48,256]{2,0,1:T(8,128)(2,1)S(1)} %bitcast.203, s32[1024]{0:T(1024)S(1)} %pad_clamp_fusion), kind=kCustom, calls=%fused_computation.4.clone | custom fusion | bytes 5243200 | tf_op jit(solution)/shard_map/jit(_take)/gather | solution.py:58
  166.2 2.0 %broadcast_select_fusion = bf16[80,64,256]{2,1,0:T(8,128)(2,1)S(1)} fusion(bf16[80,64,256]{2,1,0:T(8,128)(2,1)} %gather_fusion.4, pred[80]{0:T(512)(128)(4,1)S(1)} %compare_and_fusion.1), kind=kLoop, calls=%fused_computation.27 | loop fusion | flops 1310720 | bytes 5242960 | tf_op jit(solution)/shard_map/jit(_take)/select_n | solution.py:58
  168.2 7.4 %fusion.39 = f32[16,8,8,256]{3,2,1,0:T(8,128)S(1)} fusion(bf16[16,5,256,256]{3,2,1,0:T(8,128)(2,1)} %param.11, bf16[64,16,5,256]{3,0,2,1:T(8,128)(2,1)S(1)} %bitcast.208, pred[16,5]{1,0:T(8,128)(4,1)S(1)} %iota_compare_fusion.5), kind=kOutput, calls=%fused_computation.66 | convolution fusion | flops 672399360 | bytes 14155856 | tf_op jit(solution)/shard_map/ijab,mijb->mia/dot_general | solution.py:62
  175.7 1.9 %fusion.2 = f32[5,64,4096]{2,1,0:T(8,128)} fusion(f32[5,64,4096]{2,1,0:T(8,128)} %get-tuple-element.14, f32[64,4096]{1,0:T(8,128)S(1)} %bitcast.218, bf16[16,32,64]{2,1,0:T(8,128)(2,1)S(1)} %reshape.196, bf16[16,32,4096]{2,1,0:T(8,128)(2,1)S(1)} %copy-done.8), kind=kOutput, calls=%fused_computation.8 | convolution fusion | flops 268697600 | bytes 6356992 | tf_op jit(solution)/shard_map/jrm,jrp->mp/dot_general | solution.py:82
  (111 shorter events, 10.4 us)
Async XLA Ops:
  0.0 31.3 %collective-permute-start.1 = (bf16[64,4096]{1,0:T(8,128)(2,1)}, bf16[64,4096]{1,0:T(8,128)(2,1)S(1)}, u32[]{:S(2)}, u32[]{:S(2)}) collective-permute-start(bf16[64,4096]{1,0:T(8,128)(2,1)} %param.10), channel_id=1, source_target_pairs={{1,0},{2,1},{3,2},{4,3},{5,4},{6,5},{7,6},{8,7},{9,8},{10,9},{11,1... | collective-permute-start | bytes 1572872 | tf_op jit(solution)/shard_map/ppermute | solution.py:18
  6.4 25.0 %collective-permute-start = (bf16[64,4096]{1,0:T(8,128)(2,1)}, bf16[64,4096]{1,0:T(8,128)(2,1)S(1)}, u32[]{:S(2)}, u32[]{:S(2)}) collective-permute-start(bf16[64,4096]{1,0:T(8,128)(2,1)} %param.10), channel_id=1, source_target_pairs={{0,1},{1,2},{2,3},{3,4},{4,5},{5,6},{6,7},{7,8},{8,9},{9,10},{10,1... | collective-permute-start | bytes 1572872 | tf_op jit(solution)/shard_map/ppermute | solution.py:16
  10.9 11.7 %copy-start.11 = (s32[16,5]{0,1:T(8,128)S(1)}, s32[16,5]{0,1:T(8,128)}, u32[]{:S(2)}) copy-start(s32[16,5]{0,1:T(8,128)} %param.12) | copy-start | bytes 964
  10.9 11.9 %copy-start.10 = (s32[32,16]{0,1:T(8,128)S(1)}, s32[32,16]{0,1:T(8,128)}, u32[]{:S(2)}) copy-start(s32[32,16]{0,1:T(8,128)} %param.14) | copy-start | bytes 6148
  10.9 12.3 %copy-start.12 = (s32[16]{0:T(128)S(1)}, s32[16]{0:T(128)}, u32[]{:S(2)}) copy-start(s32[16]{0:T(128)} %param.13) | copy-start | bytes 196
  10.9 20.4 %copy-start.9 = (bf16[64,4096]{1,0:T(8,128)(2,1)S(1)}, bf16[64,4096]{1,0:T(8,128)(2,1)}, u32[]{:S(2)}) copy-start(bf16[64,4096]{1,0:T(8,128)(2,1)} %param.10) | copy-start | bytes 1572868
  16.9 13.9 %all-to-all-start = ((bf16[32,2,1024]{2,1,0:T(2,128)(2,1)}), bf16[32,2,1024]{2,1,0:T(2,128)(2,1)S(1)}, u32[]{:S(2)}, u32[]{:S(2)}) async-start(bf16[32,2,1024]{2,1,0:T(2,128)(2,1)} %reshape.270), calls=%async_computation | async-start | bytes 262144 | tf_op jit(solution)/shard_map/all_to_all | solution.py:75
  36.1 7.5 %copy-start.4 = (bf16[16,32,4096]{2,1,0:T(8,128)(2,1)S(1)}, bf16[16,32,4096]{2,1,0:T(8,128)(2,1)}, u32[]{:S(2)}) copy-start(bf16[16,32,4096]{2,1,0:T(8,128)(2,1)} %param.17) | copy-start | bytes 12582916
  43.7 2.6 %copy-start = (bf16[16,32,4096]{2,1,0:T(8,128)(2,1)S(1)}, bf16[16,32,4096]{2,1,0:T(8,128)(2,1)}, u32[]{:S(2)}) copy-start(bf16[16,32,4096]{2,1,0:T(8,128)(2,1)} %param.16) | copy-start | bytes 12582916
  47.5 16.6 %collective-permute-start.3 = (bf16[64,4096]{1,0:T(8,128)(2,1)S(1)}, bf16[64,4096]{1,0:T(8,128)(2,1)S(1)}, u32[]{:S(2)}, u32[]{:S(2)}) collective-permute-start(bf16[64,4096]{1,0:T(8,128)(2,1)S(1)} %get-tuple-element.9), channel_id=1, source_target_pairs={{1,0},{2,1},{3,2},{4,3},{5,4},{6,5},{7,6},{8,7},{9,8},{10,9},{11,1... | collective-permute-start | bytes 1572872 | tf_op jit(solution)/shard_map/ppermute | solution.py:18
  48.7 15.4 %collective-permute-start.2 = (bf16[64,4096]{1,0:T(8,128)(2,1)S(1)}, bf16[64,4096]{1,0:T(8,128)(2,1)S(1)}, u32[]{:S(2)}, u32[]{:S(2)}) collective-permute-start(bf16[64,4096]{1,0:T(8,128)(2,1)S(1)} %get-tuple-element.9), channel_id=1, source_target_pairs={{0,1},{1,2},{2,3},{3,4},{4,5},{5,6},{6,7},{7,8},{8,9},{9,10},{10,1... | collective-permute-start | bytes 1572872 | tf_op jit(solution)/shard_map/ppermute | solution.py:16
  68.9 7.5 %copy-start.5 = (bf16[16,32,4096]{2,1,0:T(8,128)(2,1)S(1)}, bf16[16,32,4096]{2,1,0:T(8,128)(2,1)}, u32[]{:S(2)}) copy-start(bf16[16,32,4096]{2,1,0:T(8,128)(2,1)} %param.17) | copy-start | bytes 12582916
  76.4 2.6 %copy-start.1 = (bf16[16,32,4096]{2,1,0:T(8,128)(2,1)S(1)}, bf16[16,32,4096]{2,1,0:T(8,128)(2,1)}, u32[]{:S(2)}) copy-start(bf16[16,32,4096]{2,1,0:T(8,128)(2,1)} %param.16) | copy-start | bytes 12582916
  80.2 17.3 %collective-permute-start.5 = (bf16[64,4096]{1,0:T(8,128)(2,1)S(1)}, bf16[64,4096]{1,0:T(8,128)(2,1)S(1)}, u32[]{:S(2)}, u32[]{:S(2)}) collective-permute-start(bf16[64,4096]{1,0:T(8,128)(2,1)S(1)} %get-tuple-element.11), channel_id=1, source_target_pairs={{1,0},{2,1},{3,2},{4,3},{5,4},{6,5},{7,6},{8,7},{9,8},{10,9},{11,1... | collective-permute-start | bytes 1572872 | tf_op jit(solution)/shard_map/ppermute | solution.py:18
  81.9 15.6 %collective-permute-start.4 = (bf16[64,4096]{1,0:T(8,128)(2,1)S(1)}, bf16[64,4096]{1,0:T(8,128)(2,1)S(1)}, u32[]{:S(2)}, u32[]{:S(2)}) collective-permute-start(bf16[64,4096]{1,0:T(8,128)(2,1)S(1)} %get-tuple-element.11), channel_id=1, source_target_pairs={{0,1},{1,2},{2,3},{3,4},{4,5},{5,6},{6,7},{7,8},{8,9},{9,10},{10,1... | collective-permute-start | bytes 1572872 | tf_op jit(solution)/shard_map/ppermute | solution.py:16
  102.2 7.5 %copy-start.6 = (bf16[16,32,4096]{2,1,0:T(8,128)(2,1)S(1)}, bf16[16,32,4096]{2,1,0:T(8,128)(2,1)}, u32[]{:S(2)}) copy-start(bf16[16,32,4096]{2,1,0:T(8,128)(2,1)} %param.17) | copy-start | bytes 12582916
  109.8 2.6 %copy-start.2 = (bf16[16,32,4096]{2,1,0:T(8,128)(2,1)S(1)}, bf16[16,32,4096]{2,1,0:T(8,128)(2,1)}, u32[]{:S(2)}) copy-start(bf16[16,32,4096]{2,1,0:T(8,128)(2,1)} %param.16) | copy-start | bytes 12582916
  113.6 16.7 %collective-permute-start.7 = (bf16[64,4096]{1,0:T(8,128)(2,1)S(1)}, bf16[64,4096]{1,0:T(8,128)(2,1)S(1)}, u32[]{:S(2)}, u32[]{:S(2)}) collective-permute-start(bf16[64,4096]{1,0:T(8,128)(2,1)S(1)} %get-tuple-element.13), channel_id=1, source_target_pairs={{1,0},{2,1},{3,2},{4,3},{5,4},{6,5},{7,6},{8,7},{9,8},{10,9},{11,1... | collective-permute-start | bytes 1572872 | tf_op jit(solution)/shard_map/ppermute | solution.py:18
  114.9 15.4 %collective-permute-start.6 = (bf16[64,4096]{1,0:T(8,128)(2,1)S(1)}, bf16[64,4096]{1,0:T(8,128)(2,1)S(1)}, u32[]{:S(2)}, u32[]{:S(2)}) collective-permute-start(bf16[64,4096]{1,0:T(8,128)(2,1)S(1)} %get-tuple-element.13), channel_id=1, source_target_pairs={{0,1},{1,2},{2,3},{3,4},{4,5},{5,6},{6,7},{7,8},{8,9},{9,10},{10,1... | collective-permute-start | bytes 1572872 | tf_op jit(solution)/shard_map/ppermute | solution.py:16
  135.0 7.5 %copy-start.7 = (bf16[16,32,4096]{2,1,0:T(8,128)(2,1)S(1)}, bf16[16,32,4096]{2,1,0:T(8,128)(2,1)}, u32[]{:S(2)}) copy-start(bf16[16,32,4096]{2,1,0:T(8,128)(2,1)} %param.17) | copy-start | bytes 12582916
  142.6 2.6 %copy-start.3 = (bf16[16,32,4096]{2,1,0:T(8,128)(2,1)S(1)}, bf16[16,32,4096]{2,1,0:T(8,128)(2,1)}, u32[]{:S(2)}) copy-start(bf16[16,32,4096]{2,1,0:T(8,128)(2,1)} %param.16) | copy-start | bytes 12582916
  146.4 17.0 %collective-permute-start.9 = (bf16[64,4096]{1,0:T(8,128)(2,1)S(1)}, bf16[64,4096]{1,0:T(8,128)(2,1)S(1)}, u32[]{:S(2)}, u32[]{:S(2)}) collective-permute-start(bf16[64,4096]{1,0:T(8,128)(2,1)S(1)} %get-tuple-element.15), channel_id=1, source_target_pairs={{1,0},{2,1},{3,2},{4,3},{5,4},{6,5},{7,6},{8,7},{9,8},{10,9},{11,1... | collective-permute-start | bytes 1572872 | tf_op jit(solution)/shard_map/ppermute | solution.py:18
  147.9 15.5 %collective-permute-start.8 = (bf16[64,4096]{1,0:T(8,128)(2,1)S(1)}, bf16[64,4096]{1,0:T(8,128)(2,1)S(1)}, u32[]{:S(2)}, u32[]{:S(2)}) collective-permute-start(bf16[64,4096]{1,0:T(8,128)(2,1)S(1)} %get-tuple-element.15), channel_id=1, source_target_pairs={{0,1},{1,2},{2,3},{3,4},{4,5},{5,6},{6,7},{7,8},{8,9},{9,10},{10,1... | collective-permute-start | bytes 1572872 | tf_op jit(solution)/shard_map/ppermute | solution.py:16
  168.2 7.5 %copy-start.8 = (bf16[16,32,4096]{2,1,0:T(8,128)(2,1)S(1)}, bf16[16,32,4096]{2,1,0:T(8,128)(2,1)}, u32[]{:S(2)}) copy-start(bf16[16,32,4096]{2,1,0:T(8,128)(2,1)} %param.17) | copy-start | bytes 12582916
where the time goes:
time: 178 us
  matrix products  57.1 us (32%)
  blocking collectives  55.2 us (31%)
  local copies, waits for them, and re-layouts  23.2 us (13%)
  starting transfers between devices  17.9 us (10%)
  other arithmetic  16.1 us (9%)
  waiting for transfers between devices  7.52 us (4%)
    all_to_all x4, blocking collectives, apply_operator(): lax.all_to_all(outgoing, 'panels', split_axis=0, concat_axis=0, tiled=True)  55.2 us
    dot_general x5, matrix products, apply_operator(): jnp.einsum('ijab,mijb->mia', near_tiles, picked, preferred_element_type=j...  37.1 us
    ppermute x5, starting transfers between devices, extended_2(): lax.ppermute(head, axis, [((i + 1) % count, i) for i in range(count)])  12.2 us
    gather x5, local copies, waits for them, and re-layouts, apply_operator(): picked = jnp.take(extended, local_leaf.reshape(-1), axis=1)  12 us
    select_n x6, other arithmetic, apply_operator(): picked = jnp.take(extended, local_leaf.reshape(-1), axis=1)  10.2 us
    dot_general x5, matrix products, apply_operator(): jnp.einsum('jrm,jrp->mp', coef, target_factor, preferred_element_type=jnp...  9.27 us
    dot_general x5, matrix products, apply_operator(): jnp.einsum('jrp,mp->jrm', source_factor, field, preferred_element_type=jn...  8.53 us
    all_to_all x1, waiting for transfers between devices, apply_operator(): lax.all_to_all(outgoing, 'panels', split_axis=0, concat_axis=0, tiled=True)  7.5 us
  transfers between devices with their start and end apart: 11, of which 1 were waited for; matrix products, arithmetic and copies ran while one was open for 10% of the time, Pallas kernels for 0%

commit v1 on v0

v1 whole, which is shorter than its diff:
```python
import functools

import jax
import jax.numpy as jnp
from jax import lax
from jax.experimental import pallas as pl
from jax.experimental.pallas import tpu as pltpu
from jax.sharding import PartitionSpec as P

ITERS = 5
MESH = pl.DeviceIdType.MESH
NT = (((1,), (1,)), ((), ()))


def kernel(
    n,
    idx_ref,
    field_hbm,
    leaves_hbm,
    near_hbm,
    src_hbm,
    tgt_hbm,
    out_hbm,
    near,
    src,
    tgt,
    field,
    ext_a,
    ext_b,
    recv_a,
    recv_b,
    outg_a,
    outg_b,
    cbuf,
    gin,
    stage_a,
    stage_b,
    load_sem,
    out_sem,
    halo_send,
    halo_recv,
    far_send,
    far_recv,
):
    me = lax.axis_index("panels")
    right, left = lax.rem(me + 1, n), lax.rem(me + n - 1, n)
    leaves, excite, leaf = leaves_hbm.shape
    slots = near_hbm.shape[0] // leaves
    far_slots, rank, _ = cbuf.shape
    far_slots -= 1
    panels = leaves * leaf
    groups = 4 if leaves % 4 == 0 else 1
    size = leaves // groups
    exts, recvs, outgs, stages = (ext_a, ext_b), (recv_a, recv_b), (outg_a, outg_b), (stage_a, stage_b)

    loads = [
        pltpu.make_async_copy(field_hbm, field, load_sem.at[0]),
        pltpu.make_async_copy(leaves_hbm, ext_a.at[pl.ds(leaves, leaves)], load_sem.at[1]),
        pltpu.make_async_copy(src_hbm, src, load_sem.at[2]),
        pltpu.make_async_copy(tgt_hbm, tgt, load_sem.at[3]),
        pltpu.make_async_copy(near_hbm, near, load_sem.at[4]),
    ]
    for load in loads:
        load.start()

    for ext in exts:
        ext[3 * leaves] = jnp.zeros((excite, leaf), jnp.bfloat16)
    for recv in recvs:
        recv[n] = jnp.zeros((rank, excite), jnp.bfloat16)
        recv[me] = jnp.zeros((rank, excite), jnp.bfloat16)
    cbuf[far_slots] = jnp.zeros((rank, excite), jnp.bfloat16)

    barrier = pltpu.get_barrier_semaphore()

    @pl.loop(1, n)
    def _(d):
        pl.semaphore_signal(barrier, inc=1, device_id=(lax.rem(me + d, n),), device_id_type=MESH)

    pl.semaphore_wait(barrier, n - 1)

    def halo(k, g, side):
        ext = exts[k % 2]
        base = 0 if side == 0 else 2 * leaves
        return pltpu.make_async_remote_copy(
            src_ref=ext.at[pl.ds(leaves + g * size, size)],
            dst_ref=ext.at[pl.ds(base + g * size, size)],
            send_sem=halo_send.at[k % 2, side, g],
            recv_sem=halo_recv.at[k % 2, side, g],
            device_id=(right if side == 0 else left,),
            device_id_type=MESH,
        )

    def block(k, d):
        peer = lax.rem(me + d, n)
        return pltpu.make_async_remote_copy(
            src_ref=outgs[k % 2].at[peer],
            dst_ref=recvs[k % 2].at[me],
            send_sem=far_send.at[k % 2, d],
            recv_sem=far_recv.at[k % 2, d],
            device_id=(peer,),
            device_id_type=MESH,
        )

    loads[1].wait()
    for g in range(groups):
        halo(0, g, 0).start()
        halo(0, g, 1).start()
    loads[0].wait()
    loads[2].wait()

    half = src.shape[0] // 2
    rows_half = half // rank
    for k in range(ITERS):
        ext, recv, outg, stage = exts[k % 2], recvs[k % 2], outgs[k % 2], stages[k % 2]

        @pl.loop(0, 2)
        def _(h):
            part = lax.dot_general(
                src[pl.ds(pl.multiple_of(h * half, half), half), :],
                field[...],
                NT,
                preferred_element_type=jnp.float32,
            )
            cbuf[pl.ds(h * rows_half, rows_half)] = part.astype(jnp.bfloat16).reshape(rows_half, rank, excite)

        @pl.loop(0, n)
        def _(t):
            outg[t] = cbuf[idx_ref[leaves * slots + t]]

        @pl.loop(1, n)
        def _(d):
            block(k, d).start()

        if k >= 2:
            pltpu.make_async_copy(stage, out_hbm.at[k - 2], out_sem.at[k % 2]).wait()

        @pl.loop(1, n)
        def _(d):
            block(k, d).wait()

        for j in range(far_slots):
            gin[pl.ds(j * rank, rank), :] = recv[idx_ref[leaves * slots + n + j]].astype(jnp.float32)
        coef = gin[...].T.astype(jnp.bfloat16)
        if k == 0:
            loads[3].wait()

        @pl.loop(0, groups)
        def _(g):
            cols = pl.ds(pl.multiple_of(g * size * leaf, size * leaf), size * leaf)
            stage[:, cols] = jnp.dot(coef, tgt[:, cols], preferred_element_type=jnp.float32)

        if k == 0:
            loads[4].wait()
        for g in range(groups):
            halo(k, g, 0).wait()
            halo(k, g, 1).wait()

        @pl.loop(0, groups)
        def _(g):
            for u in range(size):
                i = g * size + u
                cols = pl.ds(pl.multiple_of(i * leaf, leaf), leaf)
                total = stage[:, cols]
                for j in range(slots):
                    total += lax.dot_general(
                        ext[idx_ref[i * slots + j]],
                        near[i * slots + j],
                        NT,
                        preferred_element_type=jnp.float32,
                    )
                stage[:, cols] = total
                if k < ITERS - 1:
                    rounded = total.astype(jnp.bfloat16)
                    field[:, cols] = rounded
                    exts[(k + 1) % 2][leaves + i] = rounded
            if k < ITERS - 1:

                @pl.when(g > 0)
                def _():
                    halo(k + 1, g - 1, 0).start()
                    halo(k + 1, g - 1, 1).start()

        if k < ITERS - 1:
            halo(k + 1, groups - 1, 0).start()
            halo(k + 1, groups - 1, 1).start()
        pltpu.make_async_copy(stage, out_hbm.at[k], out_sem.at[k % 2]).start()
    for k in range(max(ITERS - 2, 0), ITERS):
        pltpu.make_async_copy(stages[k % 2], out_hbm.at[k], out_sem.at[k % 2]).wait()


def shards(n, excitation, near_tiles, near_offset, near_count, far_src, far_count, source_factor, target_factor):
    excite, panels = excitation.shape
    leaves, slots, leaf, _ = near_tiles.shape
    far_slots, rank, _ = source_factor.shape
    me = lax.axis_index("panels")
    ints = jnp.int32

    own = jnp.arange(leaves, dtype=ints)[:, None] + leaves + near_offset
    near_idx = jnp.where(jnp.arange(slots, dtype=ints)[None, :] < near_count[:, None], own, 3 * leaves)
    live = jnp.arange(far_slots, dtype=ints)[None, :] < far_count[:, None]
    has = jnp.sum(((far_src == me) & live).astype(ints), axis=1)
    rows = jnp.arange(n, dtype=ints)
    before = jnp.sum(jnp.where(rows[None, :] < rows[:, None], has[None, :], 0), axis=1)
    send_idx = jnp.where(has > 0, before, far_slots)
    my_src = lax.dynamic_index_in_dim(far_src, me, 0, keepdims=False)
    my_live = lax.dynamic_index_in_dim(live, me, 0, keepdims=False)
    recv_idx = jnp.where(my_live, my_src, n)
    idx = jnp.concatenate([near_idx.reshape(-1), send_idx, recv_idx]).astype(ints)
    leaf_field = excitation.reshape(excite, leaves, leaf).transpose(1, 0, 2)

    bf, f32 = jnp.bfloat16, jnp.float32
    groups = 4 if leaves % 4 == 0 else 1
    hbm = pl.BlockSpec(memory_space=pl.ANY)
    return pl.pallas_call(
        functools.partial(kernel, n),
        out_shape=jax.ShapeDtypeStruct((ITERS, excite, panels), f32),
        in_specs=[pl.BlockSpec(memory_space=pltpu.SMEM)] + [hbm] * 5,
        out_specs=hbm,
        scratch_shapes=[
            pltpu.VMEM((leaves * slots, leaf, leaf), bf),
            pltpu.VMEM((far_slots * rank, panels), bf),
            pltpu.VMEM((far_slots * rank, panels), bf),
            pltpu.VMEM((excite, panels), bf),
            pltpu.VMEM((3 * leaves + 1, excite, leaf), bf),
            pltpu.VMEM((3 * leaves + 1, excite, leaf), bf),
            pltpu.VMEM((n + 1, rank, excite), bf),
            pltpu.VMEM((n + 1, rank, excite), bf),
            pltpu.VMEM((n, rank, excite), bf),
            pltpu.VMEM((n, rank, excite), bf),
            pltpu.VMEM((far_slots + 1, rank, excite), bf),
            pltpu.VMEM((far_slots * rank, excite), f32),
            pltpu.VMEM((excite, panels), f32),
            pltpu.VMEM((excite, panels), f32),
            pltpu.SemaphoreType.DMA((5,)),
            pltpu.SemaphoreType.DMA((2,)),
            pltpu.SemaphoreType.DMA((2, 2, groups)),
            pltpu.SemaphoreType.DMA((2, 2, groups)),
            pltpu.SemaphoreType.DMA((2, n)),
            pltpu.SemaphoreType.DMA((2, n)),
        ],
        compiler_params=pltpu.CompilerParams(
            collective_id=0, has_side_effects=True, vmem_limit_bytes=60 * 1024 * 1024
        ),
    )(
        idx,
        excitation,
        leaf_field,
        near_tiles.reshape(leaves * slots, leaf, leaf),
        source_factor.reshape(far_slots * rank, panels),
        target_factor.reshape(far_slots * rank, panels),
    )


def solution(mesh):
    in_specs = (
        P(None, "panels"),
        P("panels", None, None, None),
        P("panels", None),
        P("panels"),
        P(),
        P(),
        P(None, None, "panels"),
        P(None, None, "panels"),
    )
    return jax.shard_map(
        functools.partial(shards, mesh.shape["panels"]),
        mesh=mesh,
        in_specs=in_specs,
        out_specs=P(None, None, "panels"),
        check_vma=False,
    )
```

time: 178 us -> 124 us (0.70)
  Pallas kernels: 0 us -> 112 us
  matrix products: 57.1 us -> 0 us
  blocking collectives: 55.2 us -> 0 us
  starting transfers between devices: 17.9 us -> 0 us
  local copies, waits for them, and re-layouts: 23.2 us -> 7.51 us
  other arithmetic: 16.1 us -> 3.7 us
  waiting for transfers between devices: 7.52 us -> 0 us
    pallas_call x0 -> x1, Pallas kernels: none -> 112 us  [shards(): pl.pallas_call(functools.partial(kernel, n), out_shape=jax.ShapeDtypeStru...]
    dot_general x25 -> x0, matrix products: 57.1 us -> none  [the longest x5 37.1 us: apply_operator(): jnp.einsum('ijab,mijb->mia', near_tiles, picked, preferred_element_type=j...]
    all_to_all x4 -> x0, blocking collectives: 55.2 us -> none  [apply_operator(): lax.all_to_all(outgoing, 'panels', split_axis=0, concat_axis=0, tiled=True)]
    ppermute x10 -> x0, starting transfers between devices: 12.2 us -> none  [the longest x5 12.2 us: extended_2(): lax.ppermute(head, axis, [((i + 1) % count, i) for i in range(count)])]
    gather x5 -> x0, local copies, waits for them, and re-layouts: 12 us -> none  [apply_operator(): picked = jnp.take(extended, local_leaf.reshape(-1), axis=1)]
    select_n x6 -> x3, other arithmetic: 10.2 us -> 1.58 us  [the longest x1 0.88 us: shards(): recv_idx = jnp.where(my_live, my_src, n)]
    all_to_all x1 -> x0, waiting for transfers between devices: 7.5 us -> none  [apply_operator(): lax.all_to_all(outgoing, 'panels', split_axis=0, concat_axis=0, tiled=True)]
    all_to_all x1 -> x0, starting transfers between devices: 5.7 us -> none  [apply_operator(): lax.all_to_all(outgoing, 'panels', split_axis=0, concat_axis=0, tiled=True)]
  transfers between devices with their start and end apart: 11 -> 0, of which waited for: 1 -> 0; matrix products, arithmetic and copies ran while one was open for 10% -> 0% of each run, Pallas kernels for 0% -> 0%
where the time goes in v1:
time: 124 us; the launch traced here: 123 us
  Pallas kernels  112 us (90%)
  local copies, waits for them, and re-layouts  7.51 us (6%)
  other arithmetic  3.7 us (3%)
    pallas_call x1, Pallas kernels, shards(): pl.pallas_call(functools.partial(kernel, n), out_shape=jax.ShapeDtypeStru...  112 us
    unnamed x1, local copies, waits for them, and re-layouts  5.45 us

profile of v1, /device:TPU:0, one launch (start us, length us, event | category | flops | bytes accessed | tf_op | source)
XLA Modules:
  0.0 123.5 jit_solution(15661813580032468671)
XLA Ops:
  0.0 0.7 convert_reduce_fusion
  0.7 0.1 select_reduce_fusion
  0.9 0.7 iota_compare_fusion.1
  1.5 0.9 select_reduce_fusion.1
  2.4 0.7 add_select_fusion
  3.1 0.1 copy.12
  3.2 0.1 reshape.25
  3.3 0.6 pad_add_fusion.idx_ref
  3.9 1.9 %copy.16 = bf16[8,16,8,256]{3,2,0,1:T(8,128)(2,1)} copy(bf16[8,16,8,256]{3,2,1,0:T(8,128)(2,1)} %bitcast.13) | data formatting | bytes 1048576 | tf_op jit(solution)/shard_map/reshape | solution.py:209
  5.8 112.2 %shard_map.82 = f32[5,64,4096]{2,1,0:T(8,128)} custom-call(s32[128]{0:T(128)} %pad_add_fusion.idx_ref, bf16[64,4096]{1,0:T(8,128)(2,1)} %field_hbm.1, bf16[16,64,256]{2,1,0:T(8,128)(2,1)} %bitcast.14, bf16[80,256,256]{2,1,0:T(8,128)(2,1)} %bitcast.10, bf16[512,4096]{1,0:T(8,128)(2,1)} %bitcast.11, bf16[512,4096]{1,0:T(8,128)(2,1)} %bitcast.12), custom_call_target="tpu_custom_call" | custom-call | tf_op jit(solution)/shard_map/pallas_call | solution.py:214
  118.0 5.5 %copy.18 = f32[5,64,4096]{2,1,0:T(8,128)} copy(f32[5,64,4096]{2,1,0:T(8,128)} %shard_map.82) | data formatting | bytes 10485760
  (2 shorter events, 0.0 us)

commit v2 on v1

--- a/solution.py
+++ b/solution.py
@@ -46,8 +46,9 @@
     right, left = lax.rem(me + 1, n), lax.rem(me + n - 1, n)
     leaves, excite, leaf = leaves_hbm.shape
     slots = near_hbm.shape[0] // leaves
-    far_slots, rank, _ = cbuf.shape
+    far_slots, pack, _ = cbuf.shape
     far_slots -= 1
+    rank = src.shape[0] // far_slots
     panels = leaves * leaf
     groups = 4 if leaves % 4 == 0 else 1
     size = leaves // groups
@@ -66,9 +67,9 @@
     for ext in exts:
         ext[3 * leaves] = jnp.zeros((excite, leaf), jnp.bfloat16)
     for recv in recvs:
-        recv[n] = jnp.zeros((rank, excite), jnp.bfloat16)
-        recv[me] = jnp.zeros((rank, excite), jnp.bfloat16)
-    cbuf[far_slots] = jnp.zeros((rank, excite), jnp.bfloat16)
+        recv[n] = jnp.zeros((pack, 2 * excite), jnp.bfloat16)
+        recv[me] = jnp.zeros((pack, 2 * excite), jnp.bfloat16)
+    cbuf[far_slots] = jnp.zeros((pack, 2 * excite), jnp.bfloat16)
 
     barrier = pltpu.get_barrier_semaphore()
 
@@ -121,7 +122,9 @@
                 NT,
                 preferred_element_type=jnp.float32,
             )
-            cbuf[pl.ds(h * rows_half, rows_half)] = part.astype(jnp.bfloat16).reshape(rows_half, rank, excite)
+            part = part.reshape(rows_half, 2, pack, excite)
+            part = jnp.concatenate([part[:, 0], part[:, 1]], axis=2)
+            cbuf[pl.ds(h * rows_half, rows_half)] = part.astype(jnp.bfloat16)
 
         @pl.loop(0, n)
         def _(t):
@@ -139,7 +142,9 @@
             block(k, d).wait()
 
         for j in range(far_slots):
-            gin[pl.ds(j * rank, rank), :] = recv[idx_ref[leaves * slots + n + j]].astype(jnp.float32)
+            got = recv[idx_ref[leaves * slots + n + j]].astype(jnp.float32)
+            gin[pl.ds(j * rank, pack), :] = got[:, :excite]
+            gin[pl.ds(j * rank + pack, pack), :] = got[:, excite:]
         coef = gin[...].T.astype(jnp.bfloat16)
         if k == 0:
             loads[3].wait()
@@ -223,11 +228,11 @@
             pltpu.VMEM((excite, panels), bf),
             pltpu.VMEM((3 * leaves + 1, excite, leaf), bf),
             pltpu.VMEM((3 * leaves + 1, excite, leaf), bf),
-            pltpu.VMEM((n + 1, rank, excite), bf),
-            pltpu.VMEM((n + 1, rank, excite), bf),
-            pltpu.VMEM((n, rank, excite), bf),
-            pltpu.VMEM((n, rank, excite), bf),
-            pltpu.VMEM((far_slots + 1, rank, excite), bf),
+            pltpu.VMEM((n + 1, rank // 2, 2 * excite), bf),
+            pltpu.VMEM((n + 1, rank // 2, 2 * excite), bf),
+            pltpu.VMEM((n, rank // 2, 2 * excite), bf),
+            pltpu.VMEM((n, rank // 2, 2 * excite), bf),
+            pltpu.VMEM((far_slots + 1, rank // 2, 2 * excite), bf),
             pltpu.VMEM((far_slots * rank, excite), f32),
             pltpu.VMEM((excite, panels), f32),
             pltpu.VMEM((excite, panels), f32),

time: 124 us -> 116 us (0.935)
  Pallas kernels: 112 us -> 104 us
    pallas_call x1, Pallas kernels: 112 us -> 104 us  [shards(): pl.pallas_call(functools.partial(kernel, n), out_shape=jax.ShapeDtypeStru...]
where the time goes in v2:
time: 116 us
  Pallas kernels  104 us (90%)
  local copies, waits for them, and re-layouts  7.51 us (6%)
  other arithmetic  3.7 us (3%)
    pallas_call x1, Pallas kernels, shards(): pl.pallas_call(functools.partial(kernel, n), out_shape=jax.ShapeDtypeStru...  104 us
    unnamed x1, local copies, waits for them, and re-layouts  5.45 us

profile of v2, /device:TPU:0, one launch (start us, length us, event | category | flops | bytes accessed | tf_op | source)
XLA Modules:
  0.0 115.5 jit_solution(18120594209737806387)
XLA Ops:
  0.0 0.7 convert_reduce_fusion
  0.7 0.1 select_reduce_fusion
  0.9 0.7 iota_compare_fusion.1
  1.5 0.9 select_reduce_fusion.1
  2.4 0.7 add_select_fusion
  3.1 0.1 copy.12
  3.2 0.1 reshape.25
  3.3 0.6 pad_add_fusion.idx_ref
  3.9 1.9 %copy.16 = bf16[8,16,8,256]{3,2,0,1:T(8,128)(2,1)} copy(bf16[8,16,8,256]{3,2,1,0:T(8,128)(2,1)} %bitcast.13) | data formatting | bytes 1048576 | tf_op jit(solution)/shard_map/reshape | solution.py:214
  5.8 104.3 %shard_map.82 = f32[5,64,4096]{2,1,0:T(8,128)} custom-call(s32[128]{0:T(128)} %pad_add_fusion.idx_ref, bf16[64,4096]{1,0:T(8,128)(2,1)} %field_hbm.1, bf16[16,64,256]{2,1,0:T(8,128)(2,1)} %bitcast.14, bf16[80,256,256]{2,1,0:T(8,128)(2,1)} %bitcast.10, bf16[512,4096]{1,0:T(8,128)(2,1)} %bitcast.11, bf16[512,4096]{1,0:T(8,128)(2,1)} %bitcast.12), custom_call_target="tpu_custom_call" | custom-call | tf_op jit(solution)/shard_map/pallas_call | solution.py:219
  110.1 5.5 %copy.18 = f32[5,64,4096]{2,1,0:T(8,128)} copy(f32[5,64,4096]{2,1,0:T(8,128)} %shard_map.82) | data formatting | bytes 10485760
  (2 shorter events, 0.0 us)
